TPU v7x, 128 devices: a whole 4x4x4 slice. The times are simulated.
128 devices in a mesh: blk: 16 (over z, x_hi, core), uly: 8 (over y, x_lo).
Axes of the slice: x: 4 (x_hi: 2, x_lo: 2; x = x_hi * 2 + x_lo), y: 4, z: 4, core: 2. Of those that a mesh axis runs over, the one named last changes fastest.
Arguments:
- queries: bfloat16 [2048, 128, 128], P(('blk', 'uly')), may hold values from -8 to 8
- query_tangents: bfloat16 [2048, 128, 4, 128], P(('blk', 'uly')), may hold values from -6 to 6
- keys: bfloat16 [2048, 8, 128], P(('blk', 'uly')), may hold values from -8 to 8
- key_tangents: bfloat16 [2048, 8, 4, 128], P(('blk', 'uly')), may hold values from -6 to 6
- values: bfloat16 [2048, 8, 128], P(('blk', 'uly')), may hold values from -6 to 6
- value_tangents: bfloat16 [2048, 8, 4, 128], P(('blk', 'uly')), may hold values from -6 to 6
- span_order: int32 [32], replicated, may hold values from 0 to 31, as said below
Outputs:
- attention_out: bfloat16 [2048, 128, 128], P(('blk', 'uly'))
- tangent_out: bfloat16 [2048, 128, 4, 128], P(('blk', 'uly'))
Inputs may be any that keep to these rules, and one draw needn't show every extreme that they name: span_order is a permutation of the span positions; for every b the stored spans 2 * b and 2 * b + 1 hold positions c and 31 - c for some c.
All inputs are finite; a program needn't handle non-finite values.
Results may differ from a plain program's by a relative error of at most 0.0055.
Values may be sent and summed in bfloat16 or wider, within the bound.
No kernel may reach another device: no remote copies, remote signals or barrier semaphores. Data moves between devices by JAX's collectives and lax.ppermute only.
A program may use at most 64 MiB of HBM per device.

v0:
```python
import math
import jax
import jax.numpy as jnp
from jax import lax
from jax.sharding import PartitionSpec as P

HQ = 128
KVH = 8


def in_one_piece(arrays, axis, split_dim, concat_dim, along):
    widths = [math.prod(a.shape[along:]) for a in arrays]
    both = jnp.concatenate(
        [a.reshape(*a.shape[:along], w) for a, w in zip(arrays, widths)], axis=along
    )
    out = lax.all_to_all(both, axis, split_axis=split_dim, concat_axis=concat_dim, tiled=True)
    parts = jnp.split(out, [sum(widths[:k]) for k in range(1, len(widths))], axis=along)
    return tuple((b.reshape(*out.shape[:along], *a.shape[along:]) for a, b in zip(arrays, parts)))


def sent_together(arrays, axis, dim, along):
    columns = [a.reshape(*a.shape[:along], -1) for a in arrays]
    both = jnp.concatenate(columns, axis=along)
    out, at, finished = (lax.all_gather(both, axis, axis=dim, tiled=True), 0, [])
    for a, column in zip(arrays, columns):
        slab = out[..., at : at + column.shape[along]]
        finished.append(slab.reshape(*slab.shape[:along], *a.shape[along:]))
        at += column.shape[along]
    return tuple(finished)


def positions(stored, span_order, span_rows):
    span_ids = stored // span_rows
    table_ids = jnp.arange(span_order.shape[0], dtype=jnp.int32)
    looked_up = jnp.sum(
        jnp.where(span_ids[:, None] == table_ids[None, :], span_order[None, :], 0), axis=1
    )
    return looked_up * span_rows + stored % span_rows


def per_device(queries, query_tangents, keys, key_tangents, values, value_tangents, span_order):
    local_queries, local_tangents = (
        lax.all_to_all(queries, "uly", split_axis=1, concat_axis=0, tiled=True),
        lax.all_to_all(query_tangents, "uly", split_axis=1, concat_axis=0, tiled=True),
    )
    query_rows = local_queries.shape[0]
    span_rows = query_rows // 2
    head_size = local_queries.shape[2]
    group = HQ // KVH
    kv_local = local_queries.shape[1] // group
    probes = local_tangents.shape[2]
    scaling = head_size ** (-0.5)
    stored = lax.axis_index("blk") * query_rows + jnp.arange(query_rows, dtype=jnp.int32)
    query_places = positions(stored, span_order, span_rows)
    latest = jnp.max(query_places)
    query_heads = jnp.transpose(
        local_queries.reshape(query_rows, kv_local, group, head_size), (1, 2, 0, 3)
    )
    tangent_heads = jnp.transpose(
        local_tangents.reshape(query_rows, kv_local, group, probes, head_size), (1, 2, 3, 0, 4)
    )

    def update(carry, block):
        key_block, key_tan, value_block, value_tan, key_places = block
        running_max, totals, primal_sums, tangent_sums, shifts = carry
        visible = key_places[None, :] <= query_places[:, None]
        scores = (
            jnp.einsum("grqd,kgd->grqk", query_heads, key_block, preferred_element_type=jnp.float32)
            * scaling
        )
        scores = jnp.where(visible[None, None], scores, -1e30)
        new_max = jnp.maximum(running_max, jnp.max(scores, axis=-1))
        rescale = jnp.exp(running_max - new_max)
        weights_full = jnp.where(visible[None, None], jnp.exp(scores - new_max[..., None]), 0.0)
        weights_half = weights_full.astype(jnp.bfloat16)
        score_tan = jnp.einsum(
            "grpqd,kgd->grpqk", tangent_heads, key_block, preferred_element_type=jnp.float32
        )
        score_tan = score_tan + jnp.einsum(
            "grqd,kgpd->grpqk", query_heads, key_tan, preferred_element_type=jnp.float32
        )
        weighted = weights_full[:, :, None] * (score_tan * scaling)
        totals = totals * rescale + jnp.sum(weights_full, axis=-1)
        primal_sums = primal_sums * rescale[..., None] + jnp.einsum(
            "grqk,kgd->grqd", weights_half, value_block, preferred_element_type=jnp.float32
        )
        shifts = shifts * rescale[:, :, None] + jnp.sum(weighted, axis=-1)
        tangent_sums = tangent_sums * rescale[:, :, None, :, None]
        tangent_sums = tangent_sums + jnp.einsum(
            "grpqk,kgd->grpqd",
            weighted.astype(jnp.bfloat16),
            value_block,
            preferred_element_type=jnp.float32,
        )
        tangent_sums = tangent_sums + jnp.einsum(
            "grqk,kgpd->grpqd", weights_half, value_tan, preferred_element_type=jnp.float32
        )
        return (new_max, totals, primal_sums, tangent_sums, shifts)

    def keep_state(carry, block):
        return carry

    def visit(carry, block):
        reachable = jnp.min(block[4]) <= latest
        return (lax.cond(reachable, update, keep_state, carry, block), None)

    initial = (
        jnp.full((kv_local, group, query_rows), -1e30, jnp.float32),
        jnp.zeros((kv_local, group, query_rows), jnp.float32),
        jnp.zeros((kv_local, group, query_rows, head_size), jnp.float32),
        jnp.zeros((kv_local, group, probes, query_rows, head_size), jnp.float32),
        jnp.zeros((kv_local, group, probes, query_rows), jnp.float32),
    )
    head_keys, head_key_tan, head_values, head_value_tan = in_one_piece(
        (keys, key_tangents, values, value_tangents), "uly", 1, 0, 2
    )
    carry = initial
    key_piece, key_tan_piece, value_piece, value_tan_piece = sent_together(
        (head_keys, head_key_tan, head_values, head_value_tan), "blk", 0, 2
    )
    piece_rows = key_piece.shape[0]
    block_rows = 256
    block_total = piece_rows // block_rows
    places = positions(jnp.arange(piece_rows, dtype=jnp.int32), span_order, span_rows)
    stacked = (
        key_piece.reshape(block_total, block_rows, kv_local, head_size),
        key_tan_piece.reshape(block_total, block_rows, kv_local, probes, head_size),
        value_piece.reshape(block_total, block_rows, kv_local, head_size),
        value_tan_piece.reshape(block_total, block_rows, kv_local, probes, head_size),
        places.reshape(block_total, block_rows),
    )
    carry, unused = lax.scan(visit, carry, stacked)
    running_max, totals, primal_sums, tangent_sums, shifts = carry
    primal = primal_sums / totals[..., None]
    tangent = (
        tangent_sums / totals[:, :, None, :, None]
        - primal[:, :, None] * (shifts / totals[:, :, None])[..., None]
    )
    output_rows = jnp.transpose(primal.astype(jnp.bfloat16), (2, 0, 1, 3)).reshape(
        query_rows, kv_local * group, head_size
    )
    tangent_rows = jnp.transpose(tangent.astype(jnp.bfloat16), (3, 0, 1, 2, 4)).reshape(
        query_rows, kv_local * group, probes, head_size
    )
    attention_out, tangent_out = (
        lax.all_to_all(output_rows, "uly", split_axis=0, concat_axis=1, tiled=True),
        lax.all_to_all(tangent_rows, "uly", split_axis=0, concat_axis=1, tiled=True),
    )
    return (attention_out, tangent_out)


def solution(mesh):
    placed = (
        P(("blk", "uly"), None, None),
        P(("blk", "uly"), None, None, None),
        P(("blk", "uly"), None, None),
        P(("blk", "uly"), None, None, None),
        P(("blk", "uly"), None, None),
        P(("blk", "uly"), None, None, None),
        P(),
    )
    return jax.shard_map(
        per_device,
        mesh=mesh,
        in_specs=placed,
        out_specs=(P(("blk", "uly"), None, None), P(("blk", "uly"), None, None, None)),
        check_vma=False,
    )
```

profile of v0, /device:TPU:0, one launch (start us, length us, event | category | flops | bytes accessed | tf_op | source)
XLA Modules:
  0.0 317.2 jit_solution(10333332695281003336)
XLA Ops:
  11.0 13.5 %all_to_all.84 = bf16[16,8,1280]{2,0,1:T(8,128)(2,1)} all-to-all(bf16[16,8,1280]{2,0,1:T(8,128)(2,1)S(1)} %pad_maximum_fusion), channel_id=1, replica_groups=mesh['blk'=16,'uly'=8] {'uly'}, dimensions={1} | all-to-all | bytes 655360 | tf_op jit(solution)/shard_map/all_to_all | solution.py:16
  25.7 3.5 %all-to-all-start.1 = ((bf16[16,128,128]{2,0,1:T(8,128)(2,1)}), bf16[16,128,128]{2,0,1:T(8,128)(2,1)S(1)}, u32[]{:S(2)}, u32[]{:S(2)}) async-start(bf16[16,128,128]{2,0,1:T(8,128)(2,1)} %copy.87), calls=%async_computation.1 | async-start | bytes 1048576 | tf_op jit(solution)/shard_map/all_to_all | solution.py:43
  29.2 2.5 copy.89
  31.7 6.5 %all-to-all-done.1 = bf16[16,128,128]{2,0,1:T(8,128)(2,1)S(1)} async-done(((bf16[16,128,128]{2,0,1:T(8,128)(2,1)}), bf16[16,128,128]{2,0,1:T(8,128)(2,1)S(1)}, u32[]{:S(2)}, u32[]{:S(2)}) %all-to-all-start.1) | async-done | bytes 524320 | tf_op jit(solution)/shard_map/all_to_all | solution.py:43
  38.2 3.6 %all-to-all-start.2 = ((bf16[16,128,4,128]{3,2,0,1:T(4,128)(2,1)}), bf16[16,128,4,128]{3,2,0,1:T(4,128)(2,1)S(1)}, u32[]{:S(2)}, u32[]{:S(2)}) async-start(bf16[16,128,4,128]{3,2,0,1:T(4,128)(2,1)} %copy.89), calls=%async_computation.2 | async-start | bytes 4194304 | tf_op jit(solution)/shard_map/all_to_all | solution.py:44
  42.9 32.5 %all-to-all-done.2 = bf16[16,128,4,128]{3,2,0,1:T(4,128)(2,1)S(1)} async-done(((bf16[16,128,4,128]{3,2,0,1:T(4,128)(2,1)}), bf16[16,128,4,128]{3,2,0,1:T(4,128)(2,1)S(1)}, u32[]{:S(2)}, u32[]{:S(2)}) %all-to-all-start.2) | async-done | bytes 2097184 | tf_op jit(solution)/shard_map/all_to_all | solution.py:44
  76.7 2.2 copy.90
  78.9 11.5 %all-gather.2.cloned.1.call-done = bf16[2048,1,1280]{2,0,1:T(8,128)(2,1)} async-done(((bf16[128,1,1280]{2,0,1:T(8,128)(2,1)}), bf16[2048,1,1280]{2,0,1:T(8,128)(2,1)}) %all-gather.2.cloned.1.call-update) | async-done | bytes 5242896 | tf_op jit(solution)/shard_map/all_gather | solution.py:24
  90.5 4.6 %fusion.48 = (bf16[2048,1,512]{2,0,1:T(8,128)(2,1)}, bf16[2048,1,512]{2,0,1:T(8,128)(2,1)}) fusion(bf16[2048,1,1280]{2,0,1:T(8,128)(2,1)} %all-gather.2.cloned.1.call-done), kind=kLoop, calls=%fused_computation.81 | loop fusion | bytes 8388608 | tf_op jit(solution)/shard_map/slice | solution.py:26
  95.1 4.0 %reshape.242 = bf16[8,256,1,4,128]{4,3,1,0,2:T(4,128)(2,1)} reshape(bf16[2048,1,512]{2,0,1:T(8,128)(2,1)} %get-tuple-element.325) | data formatting | bytes 4194304 | tf_op jit(solution)/shard_map/reshape;reshape | solution.py:129
  99.0 4.2 %copy.96 = bf16[8,256,1,4,128]{1,4,3,2,0:T(8,128)(2,1)} copy(bf16[8,256,1,4,128]{4,3,1,0,2:T(4,128)(2,1)} %reshape.242) | data formatting | bytes 4194304 | tf_op jit(solution)/shard_map/while | solution.py:132
  103.2 4.0 %reshape.241 = bf16[8,256,1,4,128]{4,3,1,0,2:T(4,128)(2,1)} reshape(bf16[2048,1,512]{2,0,1:T(8,128)(2,1)} %get-tuple-element.326) | data formatting | bytes 4194304 | tf_op jit(solution)/shard_map/reshape;reshape | solution.py:127
  107.2 3.5 %copy.95 = bf16[8,256,1,4,128]{4,1,3,2,0:T(8,128)(2,1)} copy(bf16[8,256,1,4,128]{4,3,1,0,2:T(4,128)(2,1)} %reshape.241) | data formatting | bytes 4194304 | tf_op jit(solution)/shard_map/while | solution.py:132
  110.7 2.1 fusion.49
  113.9 2.5 broadcast_in_dim.80
  116.3 142.2 %while.18 = (s32[]{:T(128)}, f32[1,16,128]{2,1,0:T(8,128)S(1)}, f32[1,16,128]{2,1,0:T(8,128)S(1)}, f32[1,16,128,128]{3,2,1,0:T(8,128)}, f32[1,16,4,128,128]{4,3,...) while((s32[]{:T(128)}, f32[1,16,128]{2,1,0:T(8,128)S(1)}, ...), condition=%wide.region_10.11_spmd, body=%wide.region_3.10_spmd.sunk | while | flops 2437986560 | bytes 102954992 | solution.py:132
  118.4 15.7 %conditional.2 = ((f32[1,16,128]{2,1,0:T(8,128)S(1)}, f32[1,16,128]{2,1,0:T(8,128)S(1)}, f32[1,16,128,128]{3,2,1,0:T(8,128)}, f32[1,16,4,128,128]{4,3,2,1,0:T(8,128)}, f32[1,16,4,128]{3,2,1,0:T(4,128)S(1)})) conditional(s32[]{:T(128)} %convert_element_type.36, (f32[1,16,128]{2,1,0:T(8,128)S(1)}, f32[1,16,128]{2,1,0:T(8,128)S(1)}, ...), branch_computations={%region_5.5_spmd, %region_6.9_spmd} | conditional | flops 2437986304 | bytes 102952616 | solution.py:105
  119.7 1.9 fusion.7
  123.9 2.6 fusion.47
  126.5 2.3 fusion.1
  128.8 3.3 %bitcast_add_fusion.1 = f32[1,16,4,128,128]{4,3,2,1,0:T(8,128)S(1)} fusion(f32[16,4,128,128]{3,2,1,0:T(8,128)S(1)} %fusion.1, f32[1,16,4,128,128]{4,3,2,1,0:T(8,128)S(1)} %copy-done, f32[16,128]{1,0:T(8,128)S(1)} %get-tuple-element.313, bf16[8,256,1,4,128]{1,4,3,2,0:T(8,128)(2,1)} %get-tuple-element.190, s32[]{:T(128)} %get-tuple-element.182, ...), kind=kOutput, calls=%fused_computation.2 | convolution fusion | flops 542638080 | bytes 14991872 | tf_op jit(solution)/shard_map/while/body/eval_jaxpr/cond/branch_1_fun/grqk,kgpd->grpqd/dot_general | solution.py:95
  132.2 1.9 copy-done.1
  136.2 15.7 %conditional.2 = ((f32[1,16,128]{2,1,0:T(8,128)S(1)}, f32[1,16,128]{2,1,0:T(8,128)S(1)}, f32[1,16,128,128]{3,2,1,0:T(8,128)}, f32[1,16,4,128,128]{4,3,2,1,0:T(8,128)}, f32[1,16,4,128]{3,2,1,0:T(4,128)S(1)})) conditional(s32[]{:T(128)} %convert_element_type.36, (f32[1,16,128]{2,1,0:T(8,128)S(1)}, f32[1,16,128]{2,1,0:T(8,128)S(1)}, ...), branch_computations={%region_5.5_spmd, %region_6.9_spmd} | conditional | flops 2437986304 | bytes 102952616 | solution.py:105
  137.5 1.9 fusion.7
  141.6 2.6 fusion.47
  144.3 2.3 fusion.1
  146.6 3.3 %bitcast_add_fusion.1 = f32[1,16,4,128,128]{4,3,2,1,0:T(8,128)S(1)} fusion(f32[16,4,128,128]{3,2,1,0:T(8,128)S(1)} %fusion.1, f32[1,16,4,128,128]{4,3,2,1,0:T(8,128)S(1)} %copy-done, f32[16,128]{1,0:T(8,128)S(1)} %get-tuple-element.313, bf16[8,256,1,4,128]{1,4,3,2,0:T(8,128)(2,1)} %get-tuple-element.190, s32[]{:T(128)} %get-tuple-element.182, ...), kind=kOutput, calls=%fused_computation.2 | convolution fusion | flops 542638080 | bytes 14991872 | tf_op jit(solution)/shard_map/while/body/eval_jaxpr/cond/branch_1_fun/grqk,kgpd->grpqd/dot_general | solution.py:95
  149.9 1.9 copy-done.1
  154.0 15.7 %conditional.2 = ((f32[1,16,128]{2,1,0:T(8,128)S(1)}, f32[1,16,128]{2,1,0:T(8,128)S(1)}, f32[1,16,128,128]{3,2,1,0:T(8,128)}, f32[1,16,4,128,128]{4,3,2,1,0:T(8,128)}, f32[1,16,4,128]{3,2,1,0:T(4,128)S(1)})) conditional(s32[]{:T(128)} %convert_element_type.36, (f32[1,16,128]{2,1,0:T(8,128)S(1)}, f32[1,16,128]{2,1,0:T(8,128)S(1)}, ...), branch_computations={%region_5.5_spmd, %region_6.9_spmd} | conditional | flops 2437986304 | bytes 102952616 | solution.py:105
  159.4 2.6 fusion.47
  162.0 2.3 fusion.1
  164.3 3.3 %bitcast_add_fusion.1 = f32[1,16,4,128,128]{4,3,2,1,0:T(8,128)S(1)} fusion(f32[16,4,128,128]{3,2,1,0:T(8,128)S(1)} %fusion.1, f32[1,16,4,128,128]{4,3,2,1,0:T(8,128)S(1)} %copy-done, f32[16,128]{1,0:T(8,128)S(1)} %get-tuple-element.313, bf16[8,256,1,4,128]{1,4,3,2,0:T(8,128)(2,1)} %get-tuple-element.190, s32[]{:T(128)} %get-tuple-element.182, ...), kind=kOutput, calls=%fused_computation.2 | convolution fusion | flops 542638080 | bytes 14991872 | tf_op jit(solution)/shard_map/while/body/eval_jaxpr/cond/branch_1_fun/grqk,kgpd->grpqd/dot_general | solution.py:95
  167.7 1.9 copy-done.1
  171.8 15.7 %conditional.2 = ((f32[1,16,128]{2,1,0:T(8,128)S(1)}, f32[1,16,128]{2,1,0:T(8,128)S(1)}, f32[1,16,128,128]{3,2,1,0:T(8,128)}, f32[1,16,4,128,128]{4,3,2,1,0:T(8,128)}, f32[1,16,4,128]{3,2,1,0:T(4,128)S(1)})) conditional(s32[]{:T(128)} %convert_element_type.36, (f32[1,16,128]{2,1,0:T(8,128)S(1)}, f32[1,16,128]{2,1,0:T(8,128)S(1)}, ...), branch_computations={%region_5.5_spmd, %region_6.9_spmd} | conditional | flops 2437986304 | bytes 102952616 | solution.py:105
  177.2 2.6 fusion.47
  179.8 2.3 fusion.1
  182.1 3.3 %bitcast_add_fusion.1 = f32[1,16,4,128,128]{4,3,2,1,0:T(8,128)S(1)} fusion(f32[16,4,128,128]{3,2,1,0:T(8,128)S(1)} %fusion.1, f32[1,16,4,128,128]{4,3,2,1,0:T(8,128)S(1)} %copy-done, f32[16,128]{1,0:T(8,128)S(1)} %get-tuple-element.313, bf16[8,256,1,4,128]{1,4,3,2,0:T(8,128)(2,1)} %get-tuple-element.190, s32[]{:T(128)} %get-tuple-element.182, ...), kind=kOutput, calls=%fused_computation.2 | convolution fusion | flops 542638080 | bytes 14991872 | tf_op jit(solution)/shard_map/while/body/eval_jaxpr/cond/branch_1_fun/grqk,kgpd->grpqd/dot_general | solution.py:95
  185.5 1.9 copy-done.1
  189.5 15.7 %conditional.2 = ((f32[1,16,128]{2,1,0:T(8,128)S(1)}, f32[1,16,128]{2,1,0:T(8,128)S(1)}, f32[1,16,128,128]{3,2,1,0:T(8,128)}, f32[1,16,4,128,128]{4,3,2,1,0:T(8,128)}, f32[1,16,4,128]{3,2,1,0:T(4,128)S(1)})) conditional(s32[]{:T(128)} %convert_element_type.36, (f32[1,16,128]{2,1,0:T(8,128)S(1)}, f32[1,16,128]{2,1,0:T(8,128)S(1)}, ...), branch_computations={%region_5.5_spmd, %region_6.9_spmd} | conditional | flops 2437986304 | bytes 102952616 | solution.py:105
  195.0 2.6 fusion.47
  197.6 2.3 fusion.1
  199.9 3.3 %bitcast_add_fusion.1 = f32[1,16,4,128,128]{4,3,2,1,0:T(8,128)S(1)} fusion(f32[16,4,128,128]{3,2,1,0:T(8,128)S(1)} %fusion.1, f32[1,16,4,128,128]{4,3,2,1,0:T(8,128)S(1)} %copy-done, f32[16,128]{1,0:T(8,128)S(1)} %get-tuple-element.313, bf16[8,256,1,4,128]{1,4,3,2,0:T(8,128)(2,1)} %get-tuple-element.190, s32[]{:T(128)} %get-tuple-element.182, ...), kind=kOutput, calls=%fused_computation.2 | convolution fusion | flops 542638080 | bytes 14991872 | tf_op jit(solution)/shard_map/while/body/eval_jaxpr/cond/branch_1_fun/grqk,kgpd->grpqd/dot_general | solution.py:95
  203.3 1.9 copy-done.1
  207.3 15.7 %conditional.2 = ((f32[1,16,128]{2,1,0:T(8,128)S(1)}, f32[1,16,128]{2,1,0:T(8,128)S(1)}, f32[1,16,128,128]{3,2,1,0:T(8,128)}, f32[1,16,4,128,128]{4,3,2,1,0:T(8,128)}, f32[1,16,4,128]{3,2,1,0:T(4,128)S(1)})) conditional(s32[]{:T(128)} %convert_element_type.36, (f32[1,16,128]{2,1,0:T(8,128)S(1)}, f32[1,16,128]{2,1,0:T(8,128)S(1)}, ...), branch_computations={%region_5.5_spmd, %region_6.9_spmd} | conditional | flops 2437986304 | bytes 102952616 | solution.py:105
  212.7 2.6 fusion.47
  215.4 2.3 fusion.1
  217.7 3.3 %bitcast_add_fusion.1 = f32[1,16,4,128,128]{4,3,2,1,0:T(8,128)S(1)} fusion(f32[16,4,128,128]{3,2,1,0:T(8,128)S(1)} %fusion.1, f32[1,16,4,128,128]{4,3,2,1,0:T(8,128)S(1)} %copy-done, f32[16,128]{1,0:T(8,128)S(1)} %get-tuple-element.313, bf16[8,256,1,4,128]{1,4,3,2,0:T(8,128)(2,1)} %get-tuple-element.190, s32[]{:T(128)} %get-tuple-element.182, ...), kind=kOutput, calls=%fused_computation.2 | convolution fusion | flops 542638080 | bytes 14991872 | tf_op jit(solution)/shard_map/while/body/eval_jaxpr/cond/branch_1_fun/grqk,kgpd->grpqd/dot_general | solution.py:95
  221.0 1.9 copy-done.1
  225.1 15.7 %conditional.2 = ((f32[1,16,128]{2,1,0:T(8,128)S(1)}, f32[1,16,128]{2,1,0:T(8,128)S(1)}, f32[1,16,128,128]{3,2,1,0:T(8,128)}, f32[1,16,4,128,128]{4,3,2,1,0:T(8,128)}, f32[1,16,4,128]{3,2,1,0:T(4,128)S(1)})) conditional(s32[]{:T(128)} %convert_element_type.36, (f32[1,16,128]{2,1,0:T(8,128)S(1)}, f32[1,16,128]{2,1,0:T(8,128)S(1)}, ...), branch_computations={%region_5.5_spmd, %region_6.9_spmd} | conditional | flops 2437986304 | bytes 102952616 | solution.py:105
  230.5 2.6 fusion.47
  233.1 2.3 fusion.1
  235.5 3.3 %bitcast_add_fusion.1 = f32[1,16,4,128,128]{4,3,2,1,0:T(8,128)S(1)} fusion(f32[16,4,128,128]{3,2,1,0:T(8,128)S(1)} %fusion.1, f32[1,16,4,128,128]{4,3,2,1,0:T(8,128)S(1)} %copy-done, f32[16,128]{1,0:T(8,128)S(1)} %get-tuple-element.313, bf16[8,256,1,4,128]{1,4,3,2,0:T(8,128)(2,1)} %get-tuple-element.190, s32[]{:T(128)} %get-tuple-element.182, ...), kind=kOutput, calls=%fused_computation.2 | convolution fusion | flops 542638080 | bytes 14991872 | tf_op jit(solution)/shard_map/while/body/eval_jaxpr/cond/branch_1_fun/grqk,kgpd->grpqd/dot_general | solution.py:95
  238.8 1.9 copy-done.1
  242.9 15.7 %conditional.2 = ((f32[1,16,128]{2,1,0:T(8,128)S(1)}, f32[1,16,128]{2,1,0:T(8,128)S(1)}, f32[1,16,128,128]{3,2,1,0:T(8,128)}, f32[1,16,4,128,128]{4,3,2,1,0:T(8,128)}, f32[1,16,4,128]{3,2,1,0:T(4,128)S(1)})) conditional(s32[]{:T(128)} %convert_element_type.36, (f32[1,16,128]{2,1,0:T(8,128)S(1)}, f32[1,16,128]{2,1,0:T(8,128)S(1)}, ...), branch_computations={%region_5.5_spmd, %region_6.9_spmd} | conditional | flops 2437986304 | bytes 102952616 | solution.py:105
  248.3 2.6 fusion.47
  250.9 2.3 fusion.1
  253.2 3.3 %bitcast_add_fusion.1 = f32[1,16,4,128,128]{4,3,2,1,0:T(8,128)S(1)} fusion(f32[16,4,128,128]{3,2,1,0:T(8,128)S(1)} %fusion.1, f32[1,16,4,128,128]{4,3,2,1,0:T(8,128)S(1)} %copy-done, f32[16,128]{1,0:T(8,128)S(1)} %get-tuple-element.313, bf16[8,256,1,4,128]{1,4,3,2,0:T(8,128)(2,1)} %get-tuple-element.190, s32[]{:T(128)} %get-tuple-element.182, ...), kind=kOutput, calls=%fused_computation.2 | convolution fusion | flops 542638080 | bytes 14991872 | tf_op jit(solution)/shard_map/while/body/eval_jaxpr/cond/branch_1_fun/grqk,kgpd->grpqd/dot_general | solution.py:95
  256.6 1.9 copy-done.1
  258.7 2.8 fusion.37
  261.4 4.7 %all-to-all-start.3 = ((bf16[128,16,128]{2,1,0:T(8,128)(2,1)}), bf16[128,16,128]{2,1,0:T(8,128)(2,1)S(1)}, u32[]{:S(2)}, u32[]{:S(2)}) async-start(bf16[128,16,128]{2,1,0:T(8,128)(2,1)} %get-tuple-element.330), calls=%async_computation.3 | async-start | bytes 1048576 | tf_op jit(solution)/shard_map/all_to_all | solution.py:146
  266.7 8.4 %fusion.36 = bf16[128,16,4,128]{3,2,1,0:T(4,128)(2,1)} fusion(f32[16,4,128]{1,0,2:T(8,128)S(1)} %copy.102, f32[16,128,128]{2,0,1:T(8,128)S(1)} %get-tuple-element.329, f32[16,128]{0,1:T(8,128)S(1)} %copy.97, f32[1,16,4,128,128]{4,3,2,1,0:T(8,128)} %get-tuple-element.221), kind=kLoop, calls=%fused_computation.48 | loop fusion | flops 4194304 | bytes 7380992 | tf_op jit(solution)/shard_map/reshape | solution.py:142
  276.7 4.2 %all-to-all-start.4 = ((bf16[128,16,4,128]{3,2,1,0:T(4,128)(2,1)}), bf16[128,16,4,128]{3,2,1,0:T(4,128)(2,1)S(1)}, u32[]{:S(2)}, u32[]{:S(2)}) async-start(bf16[128,16,4,128]{3,2,1,0:T(4,128)(2,1)} %fusion.36), calls=%async_computation.4 | async-start | bytes 4194304 | tf_op jit(solution)/shard_map/all_to_all | solution.py:147
  281.7 26.0 %all-to-all-done.4 = bf16[128,16,4,128]{3,2,1,0:T(4,128)(2,1)S(1)} async-done(((bf16[128,16,4,128]{3,2,1,0:T(4,128)(2,1)}), bf16[128,16,4,128]{3,2,1,0:T(4,128)(2,1)S(1)}, u32[]{:S(2)}, u32[]{:S(2)}) %all-to-all-start.4) | async-done | bytes 2097184 | tf_op jit(solution)/shard_map/all_to_all | solution.py:147
  307.7 2.7 copy.103
  (170 shorter events, 56.3 us)
Async XLA Ops:
  7.2 17.4 %copy-start.6 = (bf16[16,128,128]{2,1,0:T(8,128)(2,1)S(1)}, bf16[16,128,128]{2,1,0:T(8,128)(2,1)}, u32[]{:S(2)}) copy-start(bf16[16,128,128]{2,1,0:T(8,128)(2,1)} %param.11) | copy-start | bytes 1572868
  7.2 83.3 %all-gather.2.cloned.1.call-start = ((), (), s32[]{:S(2)}) async-start(), calls=%async_computation.5 | async-start | bytes 5570560 | tf_op jit(solution)/shard_map/all_gather | solution.py:24
  9.8 19.4 %copy-start.5 = (bf16[16,128,4,128]{3,2,1,0:T(4,128)(2,1)S(1)}, bf16[16,128,4,128]{3,2,1,0:T(4,128)(2,1)}, u32[]{:S(2)}) copy-start(bf16[16,128,4,128]{3,2,1,0:T(4,128)(2,1)} %param.12) | copy-start | bytes 6291460
  25.7 12.5 %all-to-all-start.1 = ((bf16[16,128,128]{2,0,1:T(8,128)(2,1)}), bf16[16,128,128]{2,0,1:T(8,128)(2,1)S(1)}, u32[]{:S(2)}, u32[]{:S(2)}) async-start(bf16[16,128,128]{2,0,1:T(8,128)(2,1)} %copy.87), calls=%async_computation.1 | async-start | bytes 1048576 | tf_op jit(solution)/shard_map/all_to_all | solution.py:43
  31.7 10.2 %copy-start.7 = (s32[32]{0:T(128)S(1)}, s32[32]{0:T(128)}, u32[]{:S(2)}) copy-start(s32[32]{0:T(128)} %param.17) | copy-start | bytes 388
  38.2 37.2 %all-to-all-start.2 = ((bf16[16,128,4,128]{3,2,0,1:T(4,128)(2,1)}), bf16[16,128,4,128]{3,2,0,1:T(4,128)(2,1)S(1)}, u32[]{:S(2)}, u32[]{:S(2)}) async-start(bf16[16,128,4,128]{3,2,0,1:T(4,128)(2,1)} %copy.89), calls=%async_computation.2 | async-start | bytes 4194304 | tf_op jit(solution)/shard_map/all_to_all | solution.py:44
  75.4 1.3 copy-start.2
  118.4 1.2 copy-start.3
  121.6 1.0 copy-start.4
  126.5 2.3 copy-start
  132.1 2.0 copy-start.1
  136.2 1.2 copy-start.3
  139.4 1.0 copy-start.4
  144.2 2.3 copy-start
  149.9 2.0 copy-start.1
  154.0 1.2 copy-start.3
  157.1 1.0 copy-start.4
  162.0 2.3 copy-start
  167.7 2.0 copy-start.1
  171.8 1.2 copy-start.3
  174.9 1.0 copy-start.4
  179.8 2.3 copy-start
  185.5 2.0 copy-start.1
  189.5 1.2 copy-start.3
  192.7 1.0 copy-start.4
  197.6 2.3 copy-start
  203.2 2.0 copy-start.1
  207.3 1.2 copy-start.3
  210.5 1.0 copy-start.4
  215.3 2.3 copy-start
  221.0 2.0 copy-start.1
  225.1 1.2 copy-start.3
  228.3 1.0 copy-start.4
  233.1 2.3 copy-start
  238.8 2.0 copy-start.1
  242.9 1.2 copy-start.3
  246.0 1.0 copy-start.4
  250.9 2.3 copy-start
  256.6 2.0 copy-start.1
  261.4 15.3 %all-to-all-start.3 = ((bf16[128,16,128]{2,1,0:T(8,128)(2,1)}), bf16[128,16,128]{2,1,0:T(8,128)(2,1)S(1)}, u32[]{:S(2)}, u32[]{:S(2)}) async-start(bf16[128,16,128]{2,1,0:T(8,128)(2,1)} %get-tuple-element.330), calls=%async_computation.3 | async-start | bytes 1048576 | tf_op jit(solution)/shard_map/all_to_all | solution.py:146
  276.7 31.0 %all-to-all-start.4 = ((bf16[128,16,4,128]{3,2,1,0:T(4,128)(2,1)}), bf16[128,16,4,128]{3,2,1,0:T(4,128)(2,1)S(1)}, u32[]{:S(2)}, u32[]{:S(2)}) async-start(bf16[128,16,4,128]{3,2,1,0:T(4,128)(2,1)} %fusion.36), calls=%async_computation.4 | async-start | bytes 4194304 | tf_op jit(solution)/shard_map/all_to_all | solution.py:147
Sparse Core Ops, SparseCore 0:
  24.7 65.7 all-gather.1
where the time goes:
time: 320 us; the launch traced here: 317 us
  matrix products  94.8 us (30%)
  waiting for transfers between devices  78.1 us (24%)
  local copies, waits for them, and re-layouts  64.5 us (20%)
  other arithmetic  23.9 us (7%)
  starting transfers between devices  16.1 us (5%)
  between operations  14.2 us (4%)
  blocking collectives  13.5 us (4%)
  loops' own time  12.1 us (4%)
    all_to_all x1, waiting for transfers between devices, per_device(): lax.all_to_all(query_tangents, 'uly', split_axis=1, concat_axis=0, tiled=...  32.5 us
    dot_general x8, matrix products, update(): jnp.einsum('grqk,kgpd->grpqd', weights_half, value_tan, preferred_element...  26.7 us
    all_to_all x1, waiting for transfers between devices, per_device(): lax.all_to_all(tangent_rows, 'uly', split_axis=0, concat_axis=1, tiled=True)  26 us
    cond x72, local copies, waits for them, and re-layouts  23.5 us
    dot_general x8, matrix products, update(): jnp.einsum('grqd,kgpd->grpqk', query_heads, key_tan, preferred_element_ty...  20.7 us
    dot_general x8, matrix products, update(): jnp.einsum('grpqk,kgd->grpqd', weighted.astype(jnp.bfloat16), value_block...  18.4 us
    dot_general x8, matrix products, update(): jnp.einsum('grqk,kgd->grqd', weights_half, value_block, preferred_element...  15.3 us
    all_to_all x1, blocking collectives, in_one_piece(): lax.all_to_all(both, axis, split_axis=split_dim, concat_axis=concat_dim,...  13.5 us
  transfers between devices with their start and end apart: 5, of which 5 were waited for; matrix products, arithmetic and copies ran while one was open for 5% of the time, Pallas kernels for 0%

commit v1 on v0

--- a/solution.py
+++ b/solution.py
@@ -41,7 +41,12 @@
 def per_device(queries, query_tangents, keys, key_tangents, values, value_tangents, span_order):
     local_queries, local_tangents = (
         lax.all_to_all(queries, "uly", split_axis=1, concat_axis=0, tiled=True),
-        lax.all_to_all(query_tangents, "uly", split_axis=1, concat_axis=0, tiled=True),
+        jnp.concatenate(
+            lax.all_to_all(
+                jnp.stack(jnp.split(query_tangents, lax.axis_size("uly"), axis=1)), "uly", 0, 0
+            ),
+            axis=0,
+        ),
     )
     query_rows = local_queries.shape[0]
     span_rows = query_rows // 2

time: 320 us -> 318 us (level)
  local copies, waits for them, and re-layouts: 64.5 us -> 67.9 us
  waiting for transfers between devices: 78.1 us -> 74.7 us
    all_to_all x1, waiting for transfers between devices: 6.52 us -> 2.57 us  [per_device(): lax.all_to_all(queries, 'uly', split_axis=1, concat_axis=0, tiled=True)]
    unnamed x12 -> x16, local copies, waits for them, and re-layouts: 6.55 us -> 8.38 us
  transfers between devices with their start and end apart: 5 -> 5, of which waited for: 5 -> 5; matrix products, arithmetic and copies ran while one was open for 5% -> 7% of each run, Pallas kernels for 0% -> 0%
where the time goes in v1:
time: 318 us; the launch traced here: 316 us
  matrix products  94.8 us (30%)
  waiting for transfers between devices  74.7 us (23%)
  local copies, waits for them, and re-layouts  67.9 us (21%)
  other arithmetic  23.3 us (7%)
  starting transfers between devices  16.8 us (5%)
  between operations  14.2 us (4%)
  blocking collectives  13.5 us (4%)
  loops' own time  10.7 us (3%)
    all_to_all x1, waiting for transfers between devices, per_device(): lax.all_to_all(jnp.stack(jnp.split(query_tangents, lax.axis_size('uly'),...  33.3 us
    dot_general x8, matrix products, update(): jnp.einsum('grqk,kgpd->grpqd', weights_half, value_tan, preferred_element...  26.7 us
    all_to_all x1, waiting for transfers between devices, per_device(): lax.all_to_all(tangent_rows, 'uly', split_axis=0, concat_axis=1, tiled=True)  26 us
    cond x72, local copies, waits for them, and re-layouts  23.5 us
    dot_general x8, matrix products, update(): jnp.einsum('grqd,kgpd->grpqk', query_heads, key_tan, preferred_element_ty...  20.6 us
    dot_general x8, matrix products, update(): jnp.einsum('grpqk,kgd->grpqd', weighted.astype(jnp.bfloat16), value_block...  18.4 us
    dot_general x8, matrix products, update(): jnp.einsum('grqk,kgd->grqd', weights_half, value_block, preferred_element...  15.3 us
    all_to_all x1, blocking collectives, in_one_piece(): lax.all_to_all(both, axis, split_axis=split_dim, concat_axis=concat_dim,...  13.5 us
  transfers between devices with their start and end apart: 5, of which 5 were waited for; matrix products, arithmetic and copies ran while one was open for 7% of the time, Pallas kernels for 0%

profile of v1, /device:TPU:0, one launch (start us, length us, event | category | flops | bytes accessed | tf_op | source)
XLA Modules:
  0.0 315.8 jit_solution(9763907361583456761)
XLA Ops:
  11.0 13.5 %all_to_all.74 = bf16[16,8,1280]{2,0,1:T(8,128)(2,1)} all-to-all(bf16[16,8,1280]{2,0,1:T(8,128)(2,1)S(1)} %pad_maximum_fusion), channel_id=1, replica_groups=mesh['blk'=16,'uly'=8] {'uly'}, dimensions={1} | all-to-all | bytes 655360 | tf_op jit(solution)/shard_map/all_to_all | solution.py:16
  25.7 3.5 %all-to-all-start.1 = ((bf16[16,128,128]{2,0,1:T(8,128)(2,1)}), bf16[16,128,128]{2,0,1:T(8,128)(2,1)S(1)}, u32[]{:S(2)}, u32[]{:S(2)}) async-start(bf16[16,128,128]{2,0,1:T(8,128)(2,1)} %copy.86), calls=%async_computation.1 | async-start | bytes 1048576 | tf_op jit(solution)/shard_map/all_to_all | solution.py:43
  35.7 2.6 all-to-all-done.1
  38.2 4.4 %all-to-all-start.2 = ((bf16[8,16,16,4,128]{4,3,2,1,0:T(4,128)(2,1)}), bf16[8,16,16,4,128]{4,3,2,1,0:T(4,128)(2,1)}, u32[]{:S(2)}, u32[]{:S(2)}) async-start(bf16[8,16,16,4,128]{4,3,2,1,0:T(4,128)(2,1)} %bitcast_dynamic-update-slice_fusion), calls=%async_computation.2 | async-start | bytes 4194304 | tf_op jit(solution)/shard_map/all_to_all | solution.py:45
  43.7 33.3 %all-to-all-done.2 = bf16[8,16,16,4,128]{4,3,2,1,0:T(4,128)(2,1)} async-done(((bf16[8,16,16,4,128]{4,3,2,1,0:T(4,128)(2,1)}), bf16[8,16,16,4,128]{4,3,2,1,0:T(4,128)(2,1)}, u32[]{:S(2)}, u32[]{:S(2)}) %all-to-all-start.2) | async-done | bytes 2097184 | tf_op jit(solution)/shard_map/all_to_all | solution.py:45
  77.0 3.0 copy.88
  80.0 11.2 %all-gather.2.cloned.1.call-done = bf16[2048,1,1280]{2,0,1:T(8,128)(2,1)} async-done(((bf16[128,1,1280]{2,0,1:T(8,128)(2,1)}), bf16[2048,1,1280]{2,0,1:T(8,128)(2,1)}) %all-gather.2.cloned.1.call-update) | async-done | bytes 5242896 | tf_op jit(solution)/shard_map/all_gather | solution.py:24
  91.2 4.6 %fusion.48 = (bf16[2048,1,512]{2,0,1:T(8,128)(2,1)}, bf16[2048,1,512]{2,0,1:T(8,128)(2,1)}) fusion(bf16[2048,1,1280]{2,0,1:T(8,128)(2,1)} %all-gather.2.cloned.1.call-done), kind=kLoop, calls=%fused_computation.89 | loop fusion | bytes 8388608 | tf_op jit(solution)/shard_map/slice | solution.py:26
  95.8 4.0 %reshape.237 = bf16[8,256,1,4,128]{4,3,1,0,2:T(4,128)(2,1)} reshape(bf16[2048,1,512]{2,0,1:T(8,128)(2,1)} %get-tuple-element.325) | data formatting | bytes 4194304 | tf_op jit(solution)/shard_map/reshape;reshape | solution.py:134
  99.8 4.2 %copy.94 = bf16[8,256,1,4,128]{1,4,3,2,0:T(8,128)(2,1)} copy(bf16[8,256,1,4,128]{4,3,1,0,2:T(4,128)(2,1)} %reshape.237) | data formatting | bytes 4194304 | tf_op jit(solution)/shard_map/while | solution.py:137
  104.0 4.0 %reshape.236 = bf16[8,256,1,4,128]{4,3,1,0,2:T(4,128)(2,1)} reshape(bf16[2048,1,512]{2,0,1:T(8,128)(2,1)} %get-tuple-element.326) | data formatting | bytes 4194304 | tf_op jit(solution)/shard_map/reshape;reshape | solution.py:132
  107.9 3.5 %copy.93 = bf16[8,256,1,4,128]{4,1,3,2,0:T(8,128)(2,1)} copy(bf16[8,256,1,4,128]{4,3,1,0,2:T(4,128)(2,1)} %reshape.236) | data formatting | bytes 4194304 | tf_op jit(solution)/shard_map/while | solution.py:137
  111.5 2.1 fusion.49
  114.6 2.5 broadcast_in_dim.80
  117.1 140.1 %while.18 = (s32[]{:T(128)}, f32[1,16,128]{2,1,0:T(8,128)S(1)}, f32[1,16,128]{2,1,0:T(8,128)S(1)}, f32[1,16,128,128]{3,2,1,0:T(8,128)}, f32[1,16,4,128,128]{4,3,...) while((s32[]{:T(128)}, f32[1,16,128]{2,1,0:T(8,128)S(1)}, ...), condition=%wide.region_10.11_spmd, body=%wide.region_3.10_spmd.sunk | while | flops 2437986560 | bytes 102954992 | solution.py:137
  118.9 15.7 %conditional.2 = ((f32[1,16,128]{2,1,0:T(8,128)S(1)}, f32[1,16,128]{2,1,0:T(8,128)S(1)}, f32[1,16,128,128]{3,2,1,0:T(8,128)}, f32[1,16,4,128,128]{4,3,2,1,0:T(8,128)}, f32[1,16,4,128]{3,2,1,0:T(4,128)S(1)})) conditional(s32[]{:T(128)} %convert_element_type.36, (f32[1,16,128]{2,1,0:T(8,128)S(1)}, f32[1,16,128]{2,1,0:T(8,128)S(1)}, ...), branch_computations={%region_5.5_spmd, %region_6.9_spmd} | conditional | flops 2437986304 | bytes 102952616 | solution.py:110
  120.2 1.9 fusion.7
  124.4 2.6 fusion.47
  127.0 2.3 fusion.1
  129.3 3.3 %bitcast_add_fusion.1 = f32[1,16,4,128,128]{4,3,2,1,0:T(8,128)S(1)} fusion(f32[16,4,128,128]{3,2,1,0:T(8,128)S(1)} %fusion.1, f32[1,16,4,128,128]{4,3,2,1,0:T(8,128)S(1)} %copy-done, f32[16,128]{1,0:T(8,128)S(1)} %get-tuple-element.313, bf16[8,256,1,4,128]{1,4,3,2,0:T(8,128)(2,1)} %get-tuple-element.190, s32[]{:T(128)} %get-tuple-element.182, ...), kind=kOutput, calls=%fused_computation.2 | convolution fusion | flops 542638080 | bytes 14991872 | tf_op jit(solution)/shard_map/while/body/eval_jaxpr/cond/branch_1_fun/grqk,kgpd->grpqd/dot_general | solution.py:100
  132.7 1.9 copy-done.1
  136.4 15.7 %conditional.2 = ((f32[1,16,128]{2,1,0:T(8,128)S(1)}, f32[1,16,128]{2,1,0:T(8,128)S(1)}, f32[1,16,128,128]{3,2,1,0:T(8,128)}, f32[1,16,4,128,128]{4,3,2,1,0:T(8,128)}, f32[1,16,4,128]{3,2,1,0:T(4,128)S(1)})) conditional(s32[]{:T(128)} %convert_element_type.36, (f32[1,16,128]{2,1,0:T(8,128)S(1)}, f32[1,16,128]{2,1,0:T(8,128)S(1)}, ...), branch_computations={%region_5.5_spmd, %region_6.9_spmd} | conditional | flops 2437986304 | bytes 102952616 | solution.py:110
  137.7 1.9 fusion.7
  141.9 2.6 fusion.47
  144.5 2.3 fusion.1
  146.8 3.3 %bitcast_add_fusion.1 = f32[1,16,4,128,128]{4,3,2,1,0:T(8,128)S(1)} fusion(f32[16,4,128,128]{3,2,1,0:T(8,128)S(1)} %fusion.1, f32[1,16,4,128,128]{4,3,2,1,0:T(8,128)S(1)} %copy-done, f32[16,128]{1,0:T(8,128)S(1)} %get-tuple-element.313, bf16[8,256,1,4,128]{1,4,3,2,0:T(8,128)(2,1)} %get-tuple-element.190, s32[]{:T(128)} %get-tuple-element.182, ...), kind=kOutput, calls=%fused_computation.2 | convolution fusion | flops 542638080 | bytes 14991872 | tf_op jit(solution)/shard_map/while/body/eval_jaxpr/cond/branch_1_fun/grqk,kgpd->grpqd/dot_general | solution.py:100
  150.2 1.9 copy-done.1
  153.9 15.7 %conditional.2 = ((f32[1,16,128]{2,1,0:T(8,128)S(1)}, f32[1,16,128]{2,1,0:T(8,128)S(1)}, f32[1,16,128,128]{3,2,1,0:T(8,128)}, f32[1,16,4,128,128]{4,3,2,1,0:T(8,128)}, f32[1,16,4,128]{3,2,1,0:T(4,128)S(1)})) conditional(s32[]{:T(128)} %convert_element_type.36, (f32[1,16,128]{2,1,0:T(8,128)S(1)}, f32[1,16,128]{2,1,0:T(8,128)S(1)}, ...), branch_computations={%region_5.5_spmd, %region_6.9_spmd} | conditional | flops 2437986304 | bytes 102952616 | solution.py:110
  155.2 1.9 fusion.7
  159.4 2.6 fusion.47
  162.0 2.3 fusion.1
  164.3 3.3 %bitcast_add_fusion.1 = f32[1,16,4,128,128]{4,3,2,1,0:T(8,128)S(1)} fusion(f32[16,4,128,128]{3,2,1,0:T(8,128)S(1)} %fusion.1, f32[1,16,4,128,128]{4,3,2,1,0:T(8,128)S(1)} %copy-done, f32[16,128]{1,0:T(8,128)S(1)} %get-tuple-element.313, bf16[8,256,1,4,128]{1,4,3,2,0:T(8,128)(2,1)} %get-tuple-element.190, s32[]{:T(128)} %get-tuple-element.182, ...), kind=kOutput, calls=%fused_computation.2 | convolution fusion | flops 542638080 | bytes 14991872 | tf_op jit(solution)/shard_map/while/body/eval_jaxpr/cond/branch_1_fun/grqk,kgpd->grpqd/dot_general | solution.py:100
  167.7 1.9 copy-done.1
  171.5 15.7 %conditional.2 = ((f32[1,16,128]{2,1,0:T(8,128)S(1)}, f32[1,16,128]{2,1,0:T(8,128)S(1)}, f32[1,16,128,128]{3,2,1,0:T(8,128)}, f32[1,16,4,128,128]{4,3,2,1,0:T(8,128)}, f32[1,16,4,128]{3,2,1,0:T(4,128)S(1)})) conditional(s32[]{:T(128)} %convert_element_type.36, (f32[1,16,128]{2,1,0:T(8,128)S(1)}, f32[1,16,128]{2,1,0:T(8,128)S(1)}, ...), branch_computations={%region_5.5_spmd, %region_6.9_spmd} | conditional | flops 2437986304 | bytes 102952616 | solution.py:110
  176.9 2.6 fusion.47
  179.5 2.3 fusion.1
  181.8 3.3 %bitcast_add_fusion.1 = f32[1,16,4,128,128]{4,3,2,1,0:T(8,128)S(1)} fusion(f32[16,4,128,128]{3,2,1,0:T(8,128)S(1)} %fusion.1, f32[1,16,4,128,128]{4,3,2,1,0:T(8,128)S(1)} %copy-done, f32[16,128]{1,0:T(8,128)S(1)} %get-tuple-element.313, bf16[8,256,1,4,128]{1,4,3,2,0:T(8,128)(2,1)} %get-tuple-element.190, s32[]{:T(128)} %get-tuple-element.182, ...), kind=kOutput, calls=%fused_computation.2 | convolution fusion | flops 542638080 | bytes 14991872 | tf_op jit(solution)/shard_map/while/body/eval_jaxpr/cond/branch_1_fun/grqk,kgpd->grpqd/dot_general | solution.py:100
  185.2 1.9 copy-done.1
  189.0 15.7 %conditional.2 = ((f32[1,16,128]{2,1,0:T(8,128)S(1)}, f32[1,16,128]{2,1,0:T(8,128)S(1)}, f32[1,16,128,128]{3,2,1,0:T(8,128)}, f32[1,16,4,128,128]{4,3,2,1,0:T(8,128)}, f32[1,16,4,128]{3,2,1,0:T(4,128)S(1)})) conditional(s32[]{:T(128)} %convert_element_type.36, (f32[1,16,128]{2,1,0:T(8,128)S(1)}, f32[1,16,128]{2,1,0:T(8,128)S(1)}, ...), branch_computations={%region_5.5_spmd, %region_6.9_spmd} | conditional | flops 2437986304 | bytes 102952616 | solution.py:110
  194.4 2.6 fusion.47
  197.0 2.3 fusion.1
  199.3 3.3 %bitcast_add_fusion.1 = f32[1,16,4,128,128]{4,3,2,1,0:T(8,128)S(1)} fusion(f32[16,4,128,128]{3,2,1,0:T(8,128)S(1)} %fusion.1, f32[1,16,4,128,128]{4,3,2,1,0:T(8,128)S(1)} %copy-done, f32[16,128]{1,0:T(8,128)S(1)} %get-tuple-element.313, bf16[8,256,1,4,128]{1,4,3,2,0:T(8,128)(2,1)} %get-tuple-element.190, s32[]{:T(128)} %get-tuple-element.182, ...), kind=kOutput, calls=%fused_computation.2 | convolution fusion | flops 542638080 | bytes 14991872 | tf_op jit(solution)/shard_map/while/body/eval_jaxpr/cond/branch_1_fun/grqk,kgpd->grpqd/dot_general | solution.py:100
  202.7 1.9 copy-done.1
  206.5 15.7 %conditional.2 = ((f32[1,16,128]{2,1,0:T(8,128)S(1)}, f32[1,16,128]{2,1,0:T(8,128)S(1)}, f32[1,16,128,128]{3,2,1,0:T(8,128)}, f32[1,16,4,128,128]{4,3,2,1,0:T(8,128)}, f32[1,16,4,128]{3,2,1,0:T(4,128)S(1)})) conditional(s32[]{:T(128)} %convert_element_type.36, (f32[1,16,128]{2,1,0:T(8,128)S(1)}, f32[1,16,128]{2,1,0:T(8,128)S(1)}, ...), branch_computations={%region_5.5_spmd, %region_6.9_spmd} | conditional | flops 2437986304 | bytes 102952616 | solution.py:110
  211.9 2.6 fusion.47
  214.5 2.3 fusion.1
  216.8 3.3 %bitcast_add_fusion.1 = f32[1,16,4,128,128]{4,3,2,1,0:T(8,128)S(1)} fusion(f32[16,4,128,128]{3,2,1,0:T(8,128)S(1)} %fusion.1, f32[1,16,4,128,128]{4,3,2,1,0:T(8,128)S(1)} %copy-done, f32[16,128]{1,0:T(8,128)S(1)} %get-tuple-element.313, bf16[8,256,1,4,128]{1,4,3,2,0:T(8,128)(2,1)} %get-tuple-element.190, s32[]{:T(128)} %get-tuple-element.182, ...), kind=kOutput, calls=%fused_computation.2 | convolution fusion | flops 542638080 | bytes 14991872 | tf_op jit(solution)/shard_map/while/body/eval_jaxpr/cond/branch_1_fun/grqk,kgpd->grpqd/dot_general | solution.py:100
  220.2 1.9 copy-done.1
  224.0 15.7 %conditional.2 = ((f32[1,16,128]{2,1,0:T(8,128)S(1)}, f32[1,16,128]{2,1,0:T(8,128)S(1)}, f32[1,16,128,128]{3,2,1,0:T(8,128)}, f32[1,16,4,128,128]{4,3,2,1,0:T(8,128)}, f32[1,16,4,128]{3,2,1,0:T(4,128)S(1)})) conditional(s32[]{:T(128)} %convert_element_type.36, (f32[1,16,128]{2,1,0:T(8,128)S(1)}, f32[1,16,128]{2,1,0:T(8,128)S(1)}, ...), branch_computations={%region_5.5_spmd, %region_6.9_spmd} | conditional | flops 2437986304 | bytes 102952616 | solution.py:110
  229.4 2.6 fusion.47
  232.0 2.3 fusion.1
  234.3 3.3 %bitcast_add_fusion.1 = f32[1,16,4,128,128]{4,3,2,1,0:T(8,128)S(1)} fusion(f32[16,4,128,128]{3,2,1,0:T(8,128)S(1)} %fusion.1, f32[1,16,4,128,128]{4,3,2,1,0:T(8,128)S(1)} %copy-done, f32[16,128]{1,0:T(8,128)S(1)} %get-tuple-element.313, bf16[8,256,1,4,128]{1,4,3,2,0:T(8,128)(2,1)} %get-tuple-element.190, s32[]{:T(128)} %get-tuple-element.182, ...), kind=kOutput, calls=%fused_computation.2 | convolution fusion | flops 542638080 | bytes 14991872 | tf_op jit(solution)/shard_map/while/body/eval_jaxpr/cond/branch_1_fun/grqk,kgpd->grpqd/dot_general | solution.py:100
  237.7 1.9 copy-done.1
  241.5 15.7 %conditional.2 = ((f32[1,16,128]{2,1,0:T(8,128)S(1)}, f32[1,16,128]{2,1,0:T(8,128)S(1)}, f32[1,16,128,128]{3,2,1,0:T(8,128)}, f32[1,16,4,128,128]{4,3,2,1,0:T(8,128)}, f32[1,16,4,128]{3,2,1,0:T(4,128)S(1)})) conditional(s32[]{:T(128)} %convert_element_type.36, (f32[1,16,128]{2,1,0:T(8,128)S(1)}, f32[1,16,128]{2,1,0:T(8,128)S(1)}, ...), branch_computations={%region_5.5_spmd, %region_6.9_spmd} | conditional | flops 2437986304 | bytes 102952616 | solution.py:110
  246.9 2.6 fusion.47
  249.5 2.3 fusion.1
  251.8 3.3 %bitcast_add_fusion.1 = f32[1,16,4,128,128]{4,3,2,1,0:T(8,128)S(1)} fusion(f32[16,4,128,128]{3,2,1,0:T(8,128)S(1)} %fusion.1, f32[1,16,4,128,128]{4,3,2,1,0:T(8,128)S(1)} %copy-done, f32[16,128]{1,0:T(8,128)S(1)} %get-tuple-element.313, bf16[8,256,1,4,128]{1,4,3,2,0:T(8,128)(2,1)} %get-tuple-element.190, s32[]{:T(128)} %get-tuple-element.182, ...), kind=kOutput, calls=%fused_computation.2 | convolution fusion | flops 542638080 | bytes 14991872 | tf_op jit(solution)/shard_map/while/body/eval_jaxpr/cond/branch_1_fun/grqk,kgpd->grpqd/dot_general | solution.py:100
  255.2 1.9 copy-done.1
  257.3 2.8 fusion.37
  260.0 4.7 %all-to-all-start.3 = ((bf16[128,16,128]{2,1,0:T(8,128)(2,1)}), bf16[128,16,128]{2,1,0:T(8,128)(2,1)S(1)}, u32[]{:S(2)}, u32[]{:S(2)}) async-start(bf16[128,16,128]{2,1,0:T(8,128)(2,1)} %get-tuple-element.330), calls=%async_computation.3 | async-start | bytes 1048576 | tf_op jit(solution)/shard_map/all_to_all | solution.py:151
  265.3 8.4 %fusion.36 = bf16[128,16,4,128]{3,2,1,0:T(4,128)(2,1)} fusion(f32[16,4,128]{1,0,2:T(8,128)S(1)} %copy.100, f32[16,128,128]{2,0,1:T(8,128)S(1)} %get-tuple-element.329, f32[16,128]{0,1:T(8,128)S(1)} %copy.95, f32[1,16,4,128,128]{4,3,2,1,0:T(8,128)} %get-tuple-element.221), kind=kLoop, calls=%fused_computation.48 | loop fusion | flops 4194304 | bytes 7380992 | tf_op jit(solution)/shard_map/reshape | solution.py:147
  275.3 4.2 %all-to-all-start.4 = ((bf16[128,16,4,128]{3,2,1,0:T(4,128)(2,1)}), bf16[128,16,4,128]{3,2,1,0:T(4,128)(2,1)S(1)}, u32[]{:S(2)}, u32[]{:S(2)}) async-start(bf16[128,16,4,128]{3,2,1,0:T(4,128)(2,1)} %fusion.36), calls=%async_computation.4 | async-start | bytes 4194304 | tf_op jit(solution)/shard_map/all_to_all | solution.py:152
  280.3 26.0 %all-to-all-done.4 = bf16[128,16,4,128]{3,2,1,0:T(4,128)(2,1)S(1)} async-done(((bf16[128,16,4,128]{3,2,1,0:T(4,128)(2,1)}), bf16[128,16,4,128]{3,2,1,0:T(4,128)(2,1)S(1)}, u32[]{:S(2)}, u32[]{:S(2)}) %all-to-all-start.4) | async-done | bytes 2097184 | tf_op jit(solution)/shard_map/all_to_all | solution.py:152
  306.3 2.7 copy.101
  (175 shorter events, 58.9 us)
Async XLA Ops:
  7.2 17.4 %copy-start.5 = (bf16[16,128,128]{2,1,0:T(8,128)(2,1)S(1)}, bf16[16,128,128]{2,1,0:T(8,128)(2,1)}, u32[]{:S(2)}) copy-start(bf16[16,128,128]{2,1,0:T(8,128)(2,1)} %param.11) | copy-start | bytes 1572868
  7.2 84.0 %all-gather.2.cloned.1.call-start = ((), (), s32[]{:S(2)}) async-start(), calls=%async_computation.5 | async-start | bytes 5570560 | tf_op jit(solution)/shard_map/all_gather | solution.py:24
  9.8 19.4 %copy-start.4 = (bf16[16,128,4,128]{3,2,1,0:T(4,128)(2,1)S(1)}, bf16[16,128,4,128]{3,2,1,0:T(4,128)(2,1)}, u32[]{:S(2)}) copy-start(bf16[16,128,4,128]{3,2,1,0:T(4,128)(2,1)} %param.12) | copy-start | bytes 6291460
  25.7 12.5 %all-to-all-start.1 = ((bf16[16,128,128]{2,0,1:T(8,128)(2,1)}), bf16[16,128,128]{2,0,1:T(8,128)(2,1)S(1)}, u32[]{:S(2)}, u32[]{:S(2)}) async-start(bf16[16,128,128]{2,0,1:T(8,128)(2,1)} %copy.86), calls=%async_computation.1 | async-start | bytes 1048576 | tf_op jit(solution)/shard_map/all_to_all | solution.py:43
  35.7 7.0 %copy-start.6 = (s32[32]{0:T(128)S(1)}, s32[32]{0:T(128)}, u32[]{:S(2)}) copy-start(s32[32]{0:T(128)} %param.17) | copy-start | bytes 388
  38.2 38.8 %all-to-all-start.2 = ((bf16[8,16,16,4,128]{4,3,2,1,0:T(4,128)(2,1)}), bf16[8,16,16,4,128]{4,3,2,1,0:T(4,128)(2,1)}, u32[]{:S(2)}, u32[]{:S(2)}) async-start(bf16[8,16,16,4,128]{4,3,2,1,0:T(4,128)(2,1)} %bitcast_dynamic-update-slice_fusion), calls=%async_computation.2 | async-start | bytes 4194304 | tf_op jit(solution)/shard_map/all_to_all | solution.py:45
  118.9 1.2 copy-start.2
  122.1 1.0 copy-start.3
  127.0 2.3 copy-start
  132.6 1.9 copy-start.1
  136.5 1.2 copy-start.2
  139.6 1.0 copy-start.3
  144.5 2.3 copy-start
  150.1 1.9 copy-start.1
  154.0 1.2 copy-start.2
  157.1 1.0 copy-start.3
  162.0 2.3 copy-start
  167.7 1.9 copy-start.1
  171.5 1.2 copy-start.2
  174.6 1.0 copy-start.3
  179.5 2.3 copy-start
  185.2 1.9 copy-start.1
  189.0 1.2 copy-start.2
  192.1 1.0 copy-start.3
  197.0 2.3 copy-start
  202.7 1.9 copy-start.1
  206.5 1.2 copy-start.2
  209.6 1.0 copy-start.3
  214.5 2.3 copy-start
  220.2 1.9 copy-start.1
  224.0 1.2 copy-start.2
  227.1 1.0 copy-start.3
  232.0 2.3 copy-start
  237.7 1.9 copy-start.1
  241.5 1.2 copy-start.2
  244.6 1.0 copy-start.3
  249.5 2.3 copy-start
  255.2 1.9 copy-start.1
  260.0 15.2 %all-to-all-start.3 = ((bf16[128,16,128]{2,1,0:T(8,128)(2,1)}), bf16[128,16,128]{2,1,0:T(8,128)(2,1)S(1)}, u32[]{:S(2)}, u32[]{:S(2)}) async-start(bf16[128,16,128]{2,1,0:T(8,128)(2,1)} %get-tuple-element.330), calls=%async_computation.3 | async-start | bytes 1048576 | tf_op jit(solution)/shard_map/all_to_all | solution.py:151
  275.3 31.0 %all-to-all-start.4 = ((bf16[128,16,4,128]{3,2,1,0:T(4,128)(2,1)}), bf16[128,16,4,128]{3,2,1,0:T(4,128)(2,1)S(1)}, u32[]{:S(2)}, u32[]{:S(2)}) async-start(bf16[128,16,4,128]{3,2,1,0:T(4,128)(2,1)} %fusion.36), calls=%async_computation.4 | async-start | bytes 4194304 | tf_op jit(solution)/shard_map/all_to_all | solution.py:152
Sparse Core Ops, SparseCore 0:
  24.7 66.4 all-gather.1
